TPU v7x, 32 devices: a whole 2x2x4 slice. The times are simulated.
32 devices in a mesh: gx: 2 (over y), gy: 4 (over x, core), gz: 4 (over z).
Axes of the slice: x: 2, y: 2, z: 4, core: 2. Of those that a mesh axis runs over, the one named last changes fastest.
Arguments:
- halo_position: float32 [3, 16, 16, 8, 128], P(None, 'gx', 'gy', 'gz'), may hold values from 0 to 1
- halo_velocity: float32 [3, 16, 16, 8, 128], P(None, 'gx', 'gy', 'gz'), may hold values from -1 to 1
- halo_mass: float32 [16, 16, 8, 128], P('gx', 'gy', 'gz'), may hold values from 0.005 to 0.08
- cell_counts: int32 [16, 16, 8], P('gx', 'gy', 'gz'), may hold values from 1 to 128, as said below
Outputs:
- predicted: float32 [3, 16, 16, 8, 128], P(None, 'gx', 'gy', 'gz')
Inputs may be any that keep to these rules, and one draw needn't show every extreme that they name: `cell_counts`: slots of a cell from its count on hold no halo.
All inputs are finite; a program needn't handle non-finite values.
Results may differ from a plain program's by a relative error of at most 0.0001.
Values sent between devices are 32-bit elements; how exact they have to be, the bound alone decides.
No kernel may reach another device: no remote copies, remote signals or barrier semaphores. Data moves between devices by JAX's collectives and lax.ppermute only.
A program may use at most 64 MiB of HBM per device.

v0:
```python
import functools
import jax
import jax.numpy as jnp
import numpy as np
from jax import lax
from jax.experimental import pallas as pl
from jax.experimental.pallas import tpu as pltpu
from jax.sharding import PartitionSpec as P

soft_sq = 0.01
cut_sq = 0.64
near = 6.0
f32, bf16 = jnp.float32, jnp.bfloat16


def rounded(v):
    return v.astype(bf16).astype(f32)


def split3(v):
    a = rounded(v)
    rest = v - a
    b = rounded(rest)
    return a, b, rest - b


def squares(v, extra=0.0):
    a = rounded(v)
    rest = v - a
    b = rounded(rest)
    top = a * a
    top_a = rounded(top)
    low = 2.0 * a * rest + rest * rest + extra
    return (a, b, rest - b), (top_a, top - top_a, *split3(low))


def source_rows(v):
    (a, b, c), (pa, pb, pc, pd, pe) = squares(v)
    one = jnp.ones_like(v)
    return [a, one, one, pa, pb, a, b, b, a, c, one, one, one, pc, pd, pe]


def target_rows(v, extra):
    (a, b, c), (pa, pb, pc, pd, pe) = squares(v, extra)
    one = jnp.ones_like(v)
    return [-2.0 * a, pa, pb, one, one, -2.0 * b, -2.0 * a, -2.0 * b, -2.0 * c, -2.0 * a, pc, pd, pe, one, one, one]


def stage_sources(ref, i, rows, base):
    at = pl.ds(pl.multiple_of(i * 8, 8), 8)
    pieces = []
    mass = ref[3, at, :] * (1.0 / (cut_sq * cut_sq))
    sums = list(split3(mass))
    for d in range(3):
        place = ref[d, at, :] - 0.5
        pieces += source_rows(place)
        sums += list(split3(mass * place))
    for k, piece in enumerate(pieces + sums):
        rows[base + k * 8:base + k * 8 + 8, :] = piece


def staged(rows, base, j, first, count):
    return rows[pl.ds(base + first * 8 + j, count, stride=8), :]


def stage_targets(own_ref, rows, right):
    def some(i, _):
        at = pl.ds(pl.multiple_of(i * 8, 8), 8)
        for d in range(3):
            base = own_ref[d, at, :] - 0.5
            for o in range(3):
                for k, piece in enumerate(target_rows(base - float(o - 1), soft_sq if d == 2 else 0.0)):
                    rows[k * 8:k * 8 + 8, :] = piece
                for j in range(8):
                    right[i * 8 + j, d * 3 + o] = staged(rows, 0, j, 0, 16).astype(bf16)
        return 0

    lax.fori_loop(0, own_ref.shape[1] // 8, some, 0)


def weighted(left, right, moments):
    q = jnp.dot(left, right, preferred_element_type=f32)
    r = lax.rsqrt(q)
    t = jnp.maximum((cut_sq + soft_sq) - q, 0.0) * r
    w = t * t * r
    hi = w.astype(bf16)
    lo = (w - hi.astype(f32)).astype(bf16)
    return jnp.dot(
        jnp.concatenate([moments, moments], axis=1), jnp.concatenate([hi, lo], axis=0), preferred_element_type=f32
    )


def pull_kernel(plan, *refs):
    kind, group = plan
    own_ref = refs[1]
    sources = {"own": 0, "caps": 2, "rim": 5}[kind]
    at = 2 + sources
    source_refs = refs[2:at] or refs[1:2]
    before = None
    if kind == "own":
        out_ref, right = refs[at:at + 2]
    else:
        right, before, out_ref = refs[at:at + 3]
        at += 1
    rows, acc, raw, items, copied, *feats = refs[at + 2:]
    fetch = pltpu.make_async_copy(refs[0], items, copied)
    fetch.start()
    columns = own_ref.shape[1] // 2
    count = items.shape[0] // 4

    widest = jnp.zeros((), f32)
    for ref in (own_ref, *(source_refs if kind != "own" else ())):
        widest = jnp.maximum(widest, jnp.max(jnp.abs(ref[0:3] - 0.5)))
    calm = widest < near

    def read(n):
        return items[4 * n], items[4 * n + 1], items[4 * n + 2], items[4 * n + 3]

    @pl.when(calm)
    def _():
        acc[...] = jnp.zeros_like(acc)
        if kind == "own":
            left, sums = feats

            def some(i, _):
                stage_sources(own_ref, i, rows, 0)
                for j in range(8):
                    left[i * 8 + j] = staged(rows, 0, j, 0, 48).T.astype(bf16)
                    sums[i * 8 + j] = staged(rows, 0, j, 48, 16).astype(bf16)
                return 0

            lax.fori_loop(0, own_ref.shape[1] // 8, some, 0)
        elif kind == "caps":
            left_caps, sums_caps = feats

            def some(i, _):
                for side in range(2):
                    stage_sources(source_refs[side], i, rows, side * 512)
                for j in range(8):
                    both = [staged(rows, side * 512, j, 0, 48) for side in range(2)]
                    left_caps[i * 8 + j] = jnp.concatenate(both, axis=0).T.astype(bf16)
                    both = [staged(rows, side * 512, j, 48, 16) for side in range(2)]
                    sums_caps[i * 8 + j] = jnp.concatenate(both, axis=0).astype(bf16)
                return 0

            lax.fori_loop(0, source_refs[0].shape[1] // 8, some, 0)
        else:
            left, sums, left_caps, sums_caps = feats
            base = 0
            for ref in source_refs:

                def some(i, _, ref=ref, base=base):
                    stage_sources(ref, i, rows, 0)
                    for c in range(2):
                        column = base + i * 2 + c
                        for z in range(2):
                            left[column * 2 + z] = staged(rows, 0, 4 * c + 1 + z, 0, 48).T.astype(bf16)
                            sums[column * 2 + z] = staged(rows, 0, 4 * c + 1 + z, 48, 16).astype(bf16)
                        both = [staged(rows, 0, 4 * c + 3 * side, 0, 48) for side in range(2)]
                        left_caps[column] = jnp.concatenate(both, axis=0).T.astype(bf16)
                        both = [staged(rows, 0, 4 * c + 3 * side, 48, 16) for side in range(2)]
                        sums_caps[column] = jnp.concatenate(both, axis=0).astype(bf16)
                    return 0

                lax.fori_loop(0, ref.shape[1] // 8, some, 0)
                base += ref.shape[1] // 4
        if kind == "own":
            stage_targets(own_ref, rows, right)
        fetch.wait()

        def some_items(g, _):
            for k in range(group):
                column, source, ox, oy = read(g * group + k)
                me = jnp.minimum(column, columns - 1) * 2
                side = [[jnp.concatenate([right[me + t, ox], right[me + t, 3 + oy], right[me + t, 6 + oz]], axis=0)
                         for oz in range(3)] for t in range(2)]
                got = None
                zed = None
                if kind != "caps":
                    low = weighted(left[source * 2], jnp.concatenate([side[0][1], side[1][0]], axis=1), sums[source * 2])
                    high = weighted(left[source * 2 + 1], jnp.concatenate([side[0][2], side[1][1]], axis=1), sums[source * 2 + 1])
                    got = low + high
                    zed = jnp.concatenate([high[:8, :128], -low[:8, 128:]], axis=1)
                if kind != "own":
                    blank = jnp.zeros_like(side[0][0])
                    right_caps = jnp.concatenate(
                        [jnp.concatenate([side[0][0], blank], axis=1), jnp.concatenate([blank, side[1][2]], axis=1)], axis=0
                    )
                    caps = weighted(left_caps[source], right_caps, sums_caps[source])
                    caps_got = jnp.concatenate([caps[:16, :128], caps[16:, 128:]], axis=1)
                    caps_zed = jnp.concatenate([-caps[:8, :128], caps[16:24, 128:]], axis=1)
                    got = caps_got if got is None else got + caps_got
                    zed = caps_zed if zed is None else zed + caps_zed
                head = got[:8]
                for t in range(2):
                    lanes = slice(128 * t, 128 * t + 128)
                    first = pl.multiple_of((t * (columns + 1) + column) * 40, 8)
                    acc[pl.ds(first, 16), :] += got[:, lanes]
                    acc[pl.ds(first + 16, 8), :] += (ox - 1).astype(f32) * head[:, lanes]
                    acc[pl.ds(first + 24, 8), :] += (oy - 1).astype(f32) * head[:, lanes]
                    acc[pl.ds(first + 32, 8), :] += zed[:, lanes]
            return 0

        lax.fori_loop(0, count // group, some_items, 0)

        def finish(i, _):
            for t in range(2):
                def row(r):
                    return acc[pl.ds((t * (columns + 1) + i * 8) * 40 + r, 8, stride=40), :]

                spot = pl.ds(i * 16 + t, 8, stride=2)
                total = row(0) + row(1) + row(2)
                for d in range(3):
                    moment = row(3 * d + 3) + row(3 * d + 4) + row(3 * d + 5)
                    moment = moment + (row(16 + 8 * d) + row(17 + 8 * d) + row(18 + 8 * d))
                    value = moment - (own_ref[d, spot, :] - 0.5) * total
                    if before is not None:
                        value = value + before[d, spot, :]
                    out_ref[d, spot, :] = value
            return 0

        lax.fori_loop(0, columns // 8, finish, 0)

    @pl.when(jnp.logical_not(calm))
    def _():
        fetch.wait()
        raw[...] = jnp.zeros_like(raw)
        base = 0
        for ref in source_refs:

            def keep(cell, _, ref=ref, base=base):
                for d in range(4):
                    raw[base + cell, d:d + 1, :] = ref[d, pl.ds(cell, 1), :]
                return 0

            lax.fori_loop(0, ref.shape[1], keep, 0)
            base += ref.shape[1]
        out_ref[...] = before[...] if before is not None else jnp.zeros_like(out_ref)
        layers = {"own": (1, 2), "caps": (0, 3), "rim": (0, 1, 2, 3)}[kind]

        def one(n, _):
            column, source, ox, oy = read(n)

            @pl.when(column < columns)
            def _():
                for layer in layers:
                    cell = {"own": source * 2 + layer - 1, "caps": source + (layer // 3) * columns, "rim": source * 4 + layer}[kind]
                    lined = raw[cell].T
                    for t in range(2):
                        if abs(layer - 1 - t) > 1:
                            continue
                        spot = pl.ds(column * 2 + t, 1)
                        offset = ((ox - 1).astype(f32), (oy - 1).astype(f32), float(layer - 1 - t))
                        away = [(lined[:, d:d + 1] + offset[d]) - own_ref[d, spot, :] for d in range(3)]
                        q = away[0] * away[0] + away[1] * away[1] + away[2] * away[2]
                        r = lax.rsqrt(q + soft_sq)
                        taper = jnp.maximum(1.0 - q * (1.0 / cut_sq), 0.0)
                        w = lined[:, 3:4] * (r * r * r) * (taper * taper)
                        for d in range(3):
                            out_ref[d, spot, :] += jnp.sum(w * away[d], axis=0, keepdims=True)
            return 0

        lax.fori_loop(0, count, one, 0)


def listed(grid, kind):
    nx, ny = grid
    found = []
    for tx in range(nx):
        for ty in range(ny):
            for ox in range(3):
                for oy in range(3):
                    x, y = tx + ox - 1, ty + oy - 1
                    inside = 0 <= x < nx and 0 <= y < ny
                    if inside and kind != "rim":
                        found.append((tx * ny + ty, x * ny + y, ox, oy))
                    elif not inside and kind == "rim":
                        beyond = int(x >= nx)
                        if 0 <= x < nx:
                            source = x if y < 0 else nx + x
                        elif 0 <= y < ny:
                            source = 2 * nx + beyond * ny + y
                        else:
                            source = 2 * nx + 2 * ny + 2 * int(y >= ny) + beyond
                        found.append((tx * ny + ty, source, ox, oy))
    return found


def pull(kind, group, grid, own, source_arrays=(), right=None, before=None):
    nx, ny = grid
    columns = nx * ny
    items = listed(grid, kind)
    while len(items) % group:
        items.append((columns, 0, 1, 1))
    table = np.asarray(items, np.int32).reshape(-1)
    cells = sum(a.shape[1] for a in source_arrays) if source_arrays else own.shape[1]
    middle = {"own": cells, "caps": 0, "rim": cells // 2}[kind]
    capped = {"own": 0, "caps": cells // 2, "rim": cells // 4}[kind]
    feats = []
    if middle:
        feats += [pltpu.VMEM((middle, 128, 48), bf16), pltpu.VMEM((middle, 16, 128), bf16)]
    if capped:
        feats += [pltpu.VMEM((capped, 128, 96), bf16), pltpu.VMEM((capped, 32, 128), bf16)]
    args = [own, *source_arrays] + ([right, before] if source_arrays else [])
    out = jax.ShapeDtypeStruct((3, own.shape[1], 128), f32)
    made = jax.ShapeDtypeStruct((own.shape[1], 9, 16, 128), bf16)
    in_vmem = pl.BlockSpec(memory_space=pltpu.VMEM)
    pairs = len(items) * (3 if kind == "rim" else 2 if kind == "own" else 1) * 128 * 256
    return pl.pallas_call(
        functools.partial(pull_kernel, (kind, group)),
        out_shape=out if source_arrays else (out, made),
        in_specs=[pl.BlockSpec(memory_space=pltpu.HBM)] + [in_vmem] * len(args),
        out_specs=in_vmem if source_arrays else (in_vmem, in_vmem),
        scratch_shapes=[
            pltpu.VMEM((1024, 128), f32),
            pltpu.VMEM((2 * (columns + 1) * 40, 128), f32),
            pltpu.VMEM((cells, 8, 128), f32),
            pltpu.SMEM(table.shape, jnp.int32),
            pltpu.SemaphoreType.DMA,
            *feats,
        ],
        compiler_params=pltpu.CompilerParams(vmem_limit_bytes=40 * 2**20),
        cost_estimate=pl.CostEstimate(flops=pairs * 40, bytes_accessed=2**20, transcendentals=pairs),
        name="pull_" + kind,
    )(jnp.asarray(table), *args)


def rolled(axes, step, cells):
    counts = [lax.axis_size(axis) for axis in axes]
    spots = list(np.ndindex(*counts))
    perm = []
    for spot in spots:
        goal = tuple((i + d) % n for i, d, n in zip(spot, step, counts))
        perm.append((spots.index(spot), spots.index(goal)))
    return lax.ppermute(cells, axes, perm)


def rolled_x(cells, axes=("gx",), step=()):
    if lax.axis_size("gx") == 2:
        return rolled(axes, (1, *step), cells)
    return jnp.concatenate([rolled(axes, (1, *step), cells[:, :1]), rolled(axes, (-1, *step), cells[:, 1:])], axis=1)


def pull_field(own):
    grid = own.shape[1:3]
    slots = own.shape[-1]

    def lined(cells):
        return cells.reshape(4, -1, slots)

    lower = rolled(("gz",), (1,), own[:, :, :, -1:])
    upper = rolled(("gz",), (-1,), own[:, :, :, :1])
    total, right = pull("own", 22, grid, lined(own))
    lower, upper, total = lax.optimization_barrier((lower, upper, total))

    def tall(*where):
        where = (slice(None), *where)
        return jnp.concatenate([lower[where], own[where], upper[where]], axis=3)

    every, first, last = slice(None), slice(0, 1), slice(-1, None)
    front = rolled(("gy",), (1,), tall(every, last))
    back = rolled(("gy",), (-1,), tall(every, first))
    sides = rolled_x(jnp.concatenate([tall(last), tall(first)], axis=1))
    corners = [
        rolled_x(jnp.concatenate([tall(last, row), tall(first, row)], axis=1), ("gx", "gy"), (step,))
        for step, row in ((1, last), (-1, first))
    ]
    total = pull("caps", 55, grid, lined(own), [lined(lower), lined(upper)], right, total)
    rim = (front, back, sides, *corners)
    rim, total = lax.optimization_barrier((rim, total))
    total = pull("rim", 17, grid, lined(own), [lined(cells) for cells in rim], right, total)
    return total.reshape(3, *own.shape[1:])


def body(halo_position, halo_velocity, halo_mass, cell_counts):
    occupied = lax.broadcasted_iota(jnp.int32, halo_mass.shape, 3) < cell_counts[..., None]
    held_mass = jnp.where(occupied, halo_mass, 0.0)[None]
    own = lax.optimization_barrier(jnp.concatenate([halo_position, held_mass], axis=0))
    first_pull = pull_field(own)
    drifted = jnp.where(occupied[None], halo_position + halo_velocity + 0.5 * first_pull, 0.0)
    own = lax.optimization_barrier(jnp.concatenate([drifted, own[3:]], axis=0))
    second_pull = pull_field(own)
    predicted = halo_position + halo_velocity + first_pull / 3.0 + second_pull / 6.0
    return jnp.where(occupied[None], predicted, 0.0)


def solution(mesh):
    return jax.shard_map(
        body,
        mesh=mesh,
        in_specs=(
            P(None, "gx", "gy", "gz", None),
            P(None, "gx", "gy", "gz", None),
            P("gx", "gy", "gz", None),
            P("gx", "gy", "gz"),
        ),
        out_specs=P(None, "gx", "gy", "gz", None),
        check_vma=False,
    )
```

profile of v0, /device:TPU:21, one launch (start us, length us, event | category | flops | bytes accessed | tf_op | source)
XLA Modules:
  0.0 277.0 jit_solution(6009828633194761699)
XLA Ops:
  0.0 0.8 copy.11
  0.8 0.9 select_bitcast_fusion
  1.6 1.0 pad_maximum_fusion
  2.6 0.1 fusion.7
  2.7 0.2 collective-permute-start.1
  2.9 1.3 collective-permute-start
  4.2 0.1 iota_compare_fusion
  4.4 0.0 copy-start
  4.4 0.7 copy-done
  5.1 23.5 %pull_own.2 = (f32[3,64,128]{2,1,0:T(8,128)S(1)}, bf16[64,9,16,128]{3,2,1,0:T(8,128)(2,1)S(1)}) custom-call(s32[880]{0:T(1024)S(1)} %copy-done, f32[4,64,128]{2,1,0:T(8,128)S(1)} %bitcast.21), custom_call_target="tpu_custom_call" | custom-call | flops 576716800 | bytes 1048576 | tf_op jit(solution)/shard_map/pull_own/pallas_call | solution.py:309
  28.7 0.0 collective-permute-done.1
  28.7 0.0 collective-permute-done
  28.8 2.3 collective-permute-start.5
  31.2 0.1 collective-permute-start.2
  31.4 1.2 collective-permute-start.4
  32.7 0.8 collective-permute-start.3
  33.5 0.2 collective-permute-start.6
  33.7 11.6 %pull_caps.2.refs_8_ = f32[3,64,128]{2,1,0:T(8,128)S(1)} custom-call(s32[880]{0:T(1024)S(1)} %copy-done, f32[4,64,128]{2,1,0:T(8,128)S(1)} %bitcast.22, f32[4,32,128]{2,1,0:T(8,128)S(1)} %bitcast.30, f32[4,32,128]{2,1,0:T(8,128)S(1)} %bitcast.29, bf16[64,9,16,128]{3,2,1,0:T(8,128)(2,1)S(1)} %get-tuple-element.30.refs_4_.refs_7_, ...), custom_call_target="tpu_custom_call" | custom-call | flops 288358400 | bytes 1048576 | tf_op jit(solution)/shard_map/pull_caps/pallas_call | solution.py:309
  45.3 0.0 collective-permute-done.5
  45.3 0.0 collective-permute-done.6
  45.3 0.0 collective-permute-done.2
  45.3 0.0 collective-permute-done.4
  45.3 0.0 collective-permute-done.3
  45.3 0.0 copy-start.3
  45.3 0.0 copy-start.4
  45.3 0.0 copy-start.1
  45.4 11.9 %pull_rim.2 = f32[3,64,128]{2,1,0:T(8,128)S(1)} custom-call(s32[272]{0:T(512)S(1)} %copy-done.2, f32[4,64,128]{2,1,0:T(8,128)S(1)} %bitcast.23, f32[4,32,128]{2,1,0:T(8,128)S(1)} %bitcast.32, f32[4,32,128]{2,1,0:T(8,128)S(1)} %bitcast.36, f32[4,32,128]{2,1,0:T(8,128)S(1)} %bitcast.34, f32[4,8,128]{2,1,0:T(8,128)S(1)} %bitcast.38, f32[4,8,128]{2,1,0:T(8,128)S(1)} %bitcast.40, ...), custom_call_target="tpu_custom_call" | custom-call | flops 267386880 | bytes 1048576 | tf_op jit(solution)/shard_map/pull_rim/pallas_call | solution.py:309
  57.3 0.1 add_select_fusion.1
  57.4 0.1 pad_maximum_fusion.1
  57.5 0.1 fusion.3
  57.6 0.2 collective-permute-start.8
  57.9 3.0 %collective-permute-start.7 = (f32[4,8,4,1,128]{4,3,2,1,0:T(1,128)S(1)}, f32[4,8,4,1,128]{4,3,2,1,0:T(1,128)S(1)}, u32[]{:S(2)}, u32[]{:S(2)}) collective-permute-start(f32[4,8,4,1,128]{4,3,2,1,0:T(1,128)S(1)} %get-tuple-element.58), channel_id=1, source_target_pairs={{0,1},{1,2},{2,3},{3,0},{4,5},{5,6},{6,7},{7,4},{8,9},{9,10},{10,1... | collective-permute-start | bytes 196616 | tf_op jit(solution)/shard_map/ppermute | solution.py:335
  60.9 23.7 %pull_own.3 = (f32[3,64,128]{2,1,0:T(8,128)S(1)}, bf16[64,9,16,128]{3,2,1,0:T(8,128)(2,1)S(1)}) custom-call(s32[880]{0:T(1024)S(1)} %copy-done.1, f32[4,64,128]{2,1,0:T(8,128)S(1)} %bitcast.24), custom_call_target="tpu_custom_call" | custom-call | flops 576716800 | bytes 1048576 | tf_op jit(solution)/shard_map/pull_own/pallas_call | solution.py:309
  84.6 0.0 collective-permute-done.8
  84.6 0.0 collective-permute-done.7
  84.8 2.9 %collective-permute-start.12 = (f32[4,2,1,4,128]{4,3,2,1,0:T(4,128)S(1)}, f32[4,2,1,4,128]{4,3,2,1,0:T(4,128)S(1)}, u32[]{:S(2)}, u32[]{:S(2)}) collective-permute-start(f32[4,2,1,4,128]{4,3,2,1,0:T(4,128)S(1)} %maximum_maximum_fusion.4), channel_id=1, source_target_pairs={{0,20},{4,24},{8,28},{12,16},{16,4},{20,8},{24,12},{28,0},{1,21},{... | collective-permute-start | bytes 49160 | tf_op jit(solution)/shard_map/ppermute | solution.py:335
  87.7 74.6 %collective-permute-start.9 = (f32[4,8,1,4,128]{4,3,2,1,0:T(4,128)S(1)}, f32[4,8,1,4,128]{4,3,2,1,0:T(4,128)S(1)}, u32[]{:S(2)}, u32[]{:S(2)}) collective-permute-start(f32[4,8,1,4,128]{4,3,2,1,0:T(4,128)S(1)} %pad_maximum_fusion.4), channel_id=1, source_target_pairs={{0,4},{4,8},{8,12},{12,0},{1,5},{5,9},{9,13},{13,1},{2,6},{6,10},{... | collective-permute-start | bytes 196616 | tf_op jit(solution)/shard_map/ppermute | solution.py:335
  162.3 0.1 maximum_maximum_fusion.1
  162.3 1.2 collective-permute-start.11
  163.6 0.8 collective-permute-start.10
  164.5 0.1 collective-permute-start.13
  164.6 69.0 %pull_caps.3.refs_8_ = f32[3,64,128]{2,1,0:T(8,128)S(1)} custom-call(s32[880]{0:T(1024)S(1)} %copy-done.1, f32[4,64,128]{2,1,0:T(8,128)S(1)} %bitcast.25, f32[4,32,128]{2,1,0:T(8,128)S(1)} %bitcast.28, f32[4,32,128]{2,1,0:T(8,128)S(1)} %bitcast.27, bf16[64,9,16,128]{3,2,1,0:T(8,128)(2,1)S(1)} %get-tuple-element.41.refs_4_.refs_7_, ...), custom_call_target="tpu_custom_call" | custom-call | flops 288358400 | bytes 1048576 | tf_op jit(solution)/shard_map/pull_caps/pallas_call | solution.py:309
  233.6 0.0 collective-permute-done.12
  233.6 0.0 collective-permute-done.13
  233.6 0.0 collective-permute-done.9
  233.6 0.0 collective-permute-done.11
  233.7 42.6 %pull_rim.3 = f32[3,64,128]{2,1,0:T(8,128)S(1)} custom-call(s32[272]{0:T(512)S(1)} %copy-done.2, f32[4,64,128]{2,1,0:T(8,128)S(1)} %bitcast.26, f32[4,32,128]{2,1,0:T(8,128)S(1)} %bitcast.31, f32[4,32,128]{2,1,0:T(8,128)S(1)} %bitcast.35, f32[4,32,128]{2,1,0:T(8,128)S(1)} %bitcast.33, f32[4,8,128]{2,1,0:T(8,128)S(1)} %bitcast.37, f32[4,8,128]{2,1,0:T(8,128)S(1)} %bitcast.39, ...), custom_call_target="tpu_custom_call" | custom-call | flops 267386880 | bytes 1048576 | tf_op jit(solution)/shard_map/pull_rim/pallas_call | solution.py:309
  276.3 0.8 add_select_fusion
  (33 shorter events, 0.6 us)
Async XLA Ops:
  2.7 25.9 %collective-permute-start.1 = (f32[4,8,4,1,128]{4,3,2,1,0:T(1,128)S(1)}, f32[4,8,4,1,128]{4,3,2,1,0:T(1,128)S(1)}, u32[]{:S(2)}, u32[]{:S(2)}) collective-permute-start(f32[4,8,4,1,128]{4,3,2,1,0:T(1,128)S(1)} %get-tuple-element.67), channel_id=1, source_target_pairs={{0,3},{1,0},{2,1},{3,2},{4,7},{5,4},{6,5},{7,6},{8,11},{9,8},{10,9... | collective-permute-start | bytes 196616 | tf_op jit(solution)/shard_map/ppermute | solution.py:335
  2.9 25.7 %collective-permute-start = (f32[4,8,4,1,128]{4,3,2,1,0:T(1,128)S(1)}, f32[4,8,4,1,128]{4,3,2,1,0:T(1,128)S(1)}, u32[]{:S(2)}, u32[]{:S(2)}) collective-permute-start(f32[4,8,4,1,128]{4,3,2,1,0:T(1,128)S(1)} %get-tuple-element.68), channel_id=1, source_target_pairs={{0,1},{1,2},{2,3},{3,0},{4,5},{5,6},{6,7},{7,4},{8,9},{9,10},{10,1... | collective-permute-start | bytes 196616 | tf_op jit(solution)/shard_map/ppermute | solution.py:335
  4.4 0.7 copy-start
  28.8 16.5 %collective-permute-start.5 = (f32[4,2,1,4,128]{4,3,2,1,0:T(4,128)S(1)}, f32[4,2,1,4,128]{4,3,2,1,0:T(4,128)S(1)}, u32[]{:S(2)}, u32[]{:S(2)}) collective-permute-start(f32[4,2,1,4,128]{4,3,2,1,0:T(4,128)S(1)} %maximum_maximum_fusion.2), channel_id=1, source_target_pairs={{0,20},{4,24},{8,28},{12,16},{16,4},{20,8},{24,12},{28,0},{1,21},{... | collective-permute-start | bytes 49160 | tf_op jit(solution)/shard_map/ppermute | solution.py:335
  31.2 14.1 %collective-permute-start.2 = (f32[4,8,1,4,128]{4,3,2,1,0:T(4,128)S(1)}, f32[4,8,1,4,128]{4,3,2,1,0:T(4,128)S(1)}, u32[]{:S(2)}, u32[]{:S(2)}) collective-permute-start(f32[4,8,1,4,128]{4,3,2,1,0:T(4,128)S(1)} %pad_maximum_fusion.2), channel_id=1, source_target_pairs={{0,4},{4,8},{8,12},{12,0},{1,5},{5,9},{9,13},{13,1},{2,6},{6,10},{... | collective-permute-start | bytes 196616 | tf_op jit(solution)/shard_map/ppermute | solution.py:335
  31.4 13.9 %collective-permute-start.4 = (f32[4,2,4,4,128]{4,3,2,1,0:T(4,128)S(1)}, f32[4,2,4,4,128]{4,3,2,1,0:T(4,128)S(1)}, u32[]{:S(2)}, u32[]{:S(2)}) collective-permute-start(f32[4,2,4,4,128]{4,3,2,1,0:T(4,128)S(1)} %maximum_maximum_fusion), channel_id=1, source_target_pairs={{0,16},{16,0},{1,17},{17,1},{2,18},{18,2},{3,19},{19,3},{4,20},{20... | collective-permute-start | bytes 196616 | tf_op jit(solution)/shard_map/ppermute | solution.py:335
  32.7 12.6 %collective-permute-start.3 = (f32[4,8,1,4,128]{4,3,2,1,0:T(4,128)S(1)}, f32[4,8,1,4,128]{4,3,2,1,0:T(4,128)S(1)}, u32[]{:S(2)}, u32[]{:S(2)}) collective-permute-start(f32[4,8,1,4,128]{4,3,2,1,0:T(4,128)S(1)} %pad_maximum_fusion.3), channel_id=1, source_target_pairs={{0,12},{4,0},{8,4},{12,8},{1,13},{5,1},{9,5},{13,9},{2,14},{6,2},{... | collective-permute-start | bytes 196616 | tf_op jit(solution)/shard_map/ppermute | solution.py:335
  33.5 11.8 %collective-permute-start.6 = (f32[4,2,1,4,128]{4,3,2,1,0:T(4,128)S(1)}, f32[4,2,1,4,128]{4,3,2,1,0:T(4,128)S(1)}, u32[]{:S(2)}, u32[]{:S(2)}) collective-permute-start(f32[4,2,1,4,128]{4,3,2,1,0:T(4,128)S(1)} %maximum_maximum_fusion.3), channel_id=1, source_target_pairs={{0,28},{4,16},{8,20},{12,24},{16,12},{20,0},{24,4},{28,8},{1,29},{... | collective-permute-start | bytes 49160 | tf_op jit(solution)/shard_map/ppermute | solution.py:335
  33.7 11.6 %copy-start.2 = (s32[272]{0:T(512)S(1)}, s32[272]{0:T(512)}, u32[]{:S(2)}) copy-start(s32[272]{0:T(512)} %constant.15.clone.refs_0_) | copy-start | bytes 3268
  45.3 12.0 %copy-start.3 = (f32[3,8,4,2,128]{4,3,2,1,0:T(2,128)S(1)}, f32[3,8,4,2,128]{4,3,2,1,0:T(2,128)}, u32[]{:S(2)}) copy-start(f32[3,8,4,2,128]{4,3,2,1,0:T(2,128)} %param.10) | copy-start | bytes 294916
  45.3 12.0 %copy-start.4 = (f32[3,8,4,2,128]{4,3,2,1,0:T(2,128)S(1)}, f32[3,8,4,2,128]{4,3,2,1,0:T(2,128)}, u32[]{:S(2)}) copy-start(f32[3,8,4,2,128]{4,3,2,1,0:T(2,128)} %param.11) | copy-start | bytes 294916
  45.3 15.5 %copy-start.1 = (s32[880]{0:T(1024)S(1)}, s32[880]{0:T(1024)}, u32[]{:S(2)}) copy-start(s32[880]{0:T(1024)} %constant.14.clone.refs_0_) | copy-start | bytes 10564
  57.6 27.0 %collective-permute-start.8 = (f32[4,8,4,1,128]{4,3,2,1,0:T(1,128)S(1)}, f32[4,8,4,1,128]{4,3,2,1,0:T(1,128)S(1)}, u32[]{:S(2)}, u32[]{:S(2)}) collective-permute-start(f32[4,8,4,1,128]{4,3,2,1,0:T(1,128)S(1)} %get-tuple-element.57), channel_id=1, source_target_pairs={{0,3},{1,0},{2,1},{3,2},{4,7},{5,4},{6,5},{7,6},{8,11},{9,8},{10,9... | collective-permute-start | bytes 196616 | tf_op jit(solution)/shard_map/ppermute | solution.py:335
  57.9 26.7 %collective-permute-start.7 = (f32[4,8,4,1,128]{4,3,2,1,0:T(1,128)S(1)}, f32[4,8,4,1,128]{4,3,2,1,0:T(1,128)S(1)}, u32[]{:S(2)}, u32[]{:S(2)}) collective-permute-start(f32[4,8,4,1,128]{4,3,2,1,0:T(1,128)S(1)} %get-tuple-element.58), channel_id=1, source_target_pairs={{0,1},{1,2},{2,3},{3,0},{4,5},{5,6},{6,7},{7,4},{8,9},{9,10},{10,1... | collective-permute-start | bytes 196616 | tf_op jit(solution)/shard_map/ppermute | solution.py:335
  84.8 148.8 %collective-permute-start.12 = (f32[4,2,1,4,128]{4,3,2,1,0:T(4,128)S(1)}, f32[4,2,1,4,128]{4,3,2,1,0:T(4,128)S(1)}, u32[]{:S(2)}, u32[]{:S(2)}) collective-permute-start(f32[4,2,1,4,128]{4,3,2,1,0:T(4,128)S(1)} %maximum_maximum_fusion.4), channel_id=1, source_target_pairs={{0,20},{4,24},{8,28},{12,16},{16,4},{20,8},{24,12},{28,0},{1,21},{... | collective-permute-start | bytes 49160 | tf_op jit(solution)/shard_map/ppermute | solution.py:335
  87.7 146.0 %collective-permute-start.9 = (f32[4,8,1,4,128]{4,3,2,1,0:T(4,128)S(1)}, f32[4,8,1,4,128]{4,3,2,1,0:T(4,128)S(1)}, u32[]{:S(2)}, u32[]{:S(2)}) collective-permute-start(f32[4,8,1,4,128]{4,3,2,1,0:T(4,128)S(1)} %pad_maximum_fusion.4), channel_id=1, source_target_pairs={{0,4},{4,8},{8,12},{12,0},{1,5},{5,9},{9,13},{13,1},{2,6},{6,10},{... | collective-permute-start | bytes 196616 | tf_op jit(solution)/shard_map/ppermute | solution.py:335
  162.3 71.3 %collective-permute-start.11 = (f32[4,2,4,4,128]{4,3,2,1,0:T(4,128)S(1)}, f32[4,2,4,4,128]{4,3,2,1,0:T(4,128)S(1)}, u32[]{:S(2)}, u32[]{:S(2)}) collective-permute-start(f32[4,2,4,4,128]{4,3,2,1,0:T(4,128)S(1)} %maximum_maximum_fusion.1), channel_id=1, source_target_pairs={{0,16},{16,0},{1,17},{17,1},{2,18},{18,2},{3,19},{19,3},{4,20},{20... | collective-permute-start | bytes 196616 | tf_op jit(solution)/shard_map/ppermute | solution.py:335
  163.6 70.0 %collective-permute-start.10 = (f32[4,8,1,4,128]{4,3,2,1,0:T(4,128)S(1)}, f32[4,8,1,4,128]{4,3,2,1,0:T(4,128)S(1)}, u32[]{:S(2)}, u32[]{:S(2)}) collective-permute-start(f32[4,8,1,4,128]{4,3,2,1,0:T(4,128)S(1)} %pad_maximum_fusion.5), channel_id=1, source_target_pairs={{0,12},{4,0},{8,4},{12,8},{1,13},{5,1},{9,5},{13,9},{2,14},{6,2},{... | collective-permute-start | bytes 196616 | tf_op jit(solution)/shard_map/ppermute | solution.py:335
  164.5 69.1 %collective-permute-start.13 = (f32[4,2,1,4,128]{4,3,2,1,0:T(4,128)S(1)}, f32[4,2,1,4,128]{4,3,2,1,0:T(4,128)S(1)}, u32[]{:S(2)}, u32[]{:S(2)}) collective-permute-start(f32[4,2,1,4,128]{4,3,2,1,0:T(4,128)S(1)} %maximum_maximum_fusion.5), channel_id=1, source_target_pairs={{0,28},{4,16},{8,20},{12,24},{16,12},{20,0},{24,4},{28,8},{1,29},{... | collective-permute-start | bytes 49160 | tf_op jit(solution)/shard_map/ppermute | solution.py:335
where the time goes:
time: 279 us; the launch traced here: 277 us
  Pallas kernels  182 us (65%)
  starting transfers between devices  89.1 us (32%)
  other arithmetic  3.21 us (1%)
    pallas_call x6, Pallas kernels, pull(): pl.pallas_call(functools.partial(pull_kernel, (kind, group)), out_shape=o...  182 us
    ppermute x14, starting transfers between devices, rolled(): return lax.ppermute(cells, axes, perm)  89.1 us
  transfers between devices with their start and end apart: 14, of which 0 were waited for; matrix products, arithmetic and copies ran while one was open for 0% of the time, Pallas kernels for 46%

commit v1 on v0

--- a/solution.py
+++ b/solution.py
@@ -350,7 +350,7 @@
 
     lower = rolled(("gz",), (1,), own[:, :, :, -1:])
     upper = rolled(("gz",), (-1,), own[:, :, :, :1])
-    total, right = pull("own", 22, grid, lined(own))
+    total, right = pull("own", 44, grid, lined(own))
     lower, upper, total = lax.optimization_barrier((lower, upper, total))
 
     def tall(*where):
@@ -365,10 +365,10 @@
         rolled_x(jnp.concatenate([tall(last, row), tall(first, row)], axis=1), ("gx", "gy"), (step,))
         for step, row in ((1, last), (-1, first))
     ]
-    total = pull("caps", 55, grid, lined(own), [lined(lower), lined(upper)], right, total)
+    total = pull("caps", 110, grid, lined(own), [lined(lower), lined(upper)], right, total)
     rim = (front, back, sides, *corners)
     rim, total = lax.optimization_barrier((rim, total))
-    total = pull("rim", 17, grid, lined(own), [lined(cells) for cells in rim], right, total)
+    total = pull("rim", 34, grid, lined(own), [lined(cells) for cells in rim], right, total)
     return total.reshape(3, *own.shape[1:])
 
 

time: 279 us -> 279 us (level)
  the two profiles are of different devices: /device:TPU:21 before, /device:TPU:5 now
where the time goes in v1:
time: 279 us; the launch traced here: 277 us
  Pallas kernels  256 us (92%)
  starting transfers between devices  15.5 us (6%)
  other arithmetic  3.21 us (1%)
    pallas_call x6, Pallas kernels, pull(): pl.pallas_call(functools.partial(pull_kernel, (kind, group)), out_shape=o...  256 us
    ppermute x14, starting transfers between devices, rolled(): return lax.ppermute(cells, axes, perm)  15.5 us
  transfers between devices with their start and end apart: 14, of which 0 were waited for; matrix products, arithmetic and copies ran while one was open for 0% of the time, Pallas kernels for 73%

profile of v1, /device:TPU:5, one launch (start us, length us, event | category | flops | bytes accessed | tf_op | source)
XLA Modules:
  0.0 277.0 jit_solution(270892151823317805)
XLA Ops:
  0.0 0.8 copy.11
  0.8 0.9 select_bitcast_fusion
  1.6 1.0 pad_maximum_fusion
  2.6 0.1 fusion.7
  2.7 3.4 %collective-permute-start.1 = (f32[4,8,4,1,128]{4,3,2,1,0:T(1,128)S(1)}, f32[4,8,4,1,128]{4,3,2,1,0:T(1,128)S(1)}, u32[]{:S(2)}, u32[]{:S(2)}) collective-permute-start(f32[4,8,4,1,128]{4,3,2,1,0:T(1,128)S(1)} %get-tuple-element.67), channel_id=1, source_target_pairs={{0,3},{1,0},{2,1},{3,2},{4,7},{5,4},{6,5},{7,6},{8,11},{9,8},{10,9... | collective-permute-start | bytes 196616 | tf_op jit(solution)/shard_map/ppermute | solution.py:335
  6.1 0.0 collective-permute-start
  6.1 0.1 iota_compare_fusion
  6.3 0.0 copy-start
  6.3 0.7 copy-done
  7.0 22.3 %pull_own.2 = (f32[3,64,128]{2,1,0:T(8,128)S(1)}, bf16[64,9,16,128]{3,2,1,0:T(8,128)(2,1)S(1)}) custom-call(s32[880]{0:T(1024)S(1)} %copy-done, f32[4,64,128]{2,1,0:T(8,128)S(1)} %bitcast.21), custom_call_target="tpu_custom_call" | custom-call | flops 576716800 | bytes 1048576 | tf_op jit(solution)/shard_map/pull_own/pallas_call | solution.py:309
  29.3 0.0 collective-permute-done.1
  29.3 0.0 collective-permute-done
  29.4 2.0 collective-permute-start.5
  31.5 0.1 collective-permute-start.2
  31.7 1.2 collective-permute-start.4
  33.0 0.8 collective-permute-start.3
  33.9 0.2 collective-permute-start.6
  34.1 11.1 %pull_caps.2.refs_8_ = f32[3,64,128]{2,1,0:T(8,128)S(1)} custom-call(s32[880]{0:T(1024)S(1)} %copy-done, f32[4,64,128]{2,1,0:T(8,128)S(1)} %bitcast.22, f32[4,32,128]{2,1,0:T(8,128)S(1)} %bitcast.30, f32[4,32,128]{2,1,0:T(8,128)S(1)} %bitcast.29, bf16[64,9,16,128]{3,2,1,0:T(8,128)(2,1)S(1)} %get-tuple-element.30.refs_4_.refs_7_, ...), custom_call_target="tpu_custom_call" | custom-call | flops 288358400 | bytes 1048576 | tf_op jit(solution)/shard_map/pull_caps/pallas_call | solution.py:309
  45.2 0.0 collective-permute-done.5
  45.2 0.0 collective-permute-done.6
  45.2 0.0 collective-permute-done.2
  45.2 0.0 collective-permute-done.4
  45.2 0.0 collective-permute-done.3
  45.2 0.0 copy-start.3
  45.2 0.0 copy-start.4
  45.2 0.0 copy-start.1
  45.3 11.6 %pull_rim.2 = f32[3,64,128]{2,1,0:T(8,128)S(1)} custom-call(s32[272]{0:T(512)S(1)} %copy-done.2, f32[4,64,128]{2,1,0:T(8,128)S(1)} %bitcast.23, f32[4,32,128]{2,1,0:T(8,128)S(1)} %bitcast.32, f32[4,32,128]{2,1,0:T(8,128)S(1)} %bitcast.36, f32[4,32,128]{2,1,0:T(8,128)S(1)} %bitcast.34, f32[4,8,128]{2,1,0:T(8,128)S(1)} %bitcast.38, f32[4,8,128]{2,1,0:T(8,128)S(1)} %bitcast.40, ...), custom_call_target="tpu_custom_call" | custom-call | flops 267386880 | bytes 1048576 | tf_op jit(solution)/shard_map/pull_rim/pallas_call | solution.py:309
  56.9 0.1 add_select_fusion.1
  57.0 0.1 pad_maximum_fusion.1
  57.1 0.1 fusion.3
  57.2 3.6 %collective-permute-start.8 = (f32[4,8,4,1,128]{4,3,2,1,0:T(1,128)S(1)}, f32[4,8,4,1,128]{4,3,2,1,0:T(1,128)S(1)}, u32[]{:S(2)}, u32[]{:S(2)}) collective-permute-start(f32[4,8,4,1,128]{4,3,2,1,0:T(1,128)S(1)} %get-tuple-element.57), channel_id=1, source_target_pairs={{0,3},{1,0},{2,1},{3,2},{4,7},{5,4},{6,5},{7,6},{8,11},{9,8},{10,9... | collective-permute-start | bytes 196616 | tf_op jit(solution)/shard_map/ppermute | solution.py:335
  60.8 0.0 collective-permute-start.7
  60.8 99.2 %pull_own.3 = (f32[3,64,128]{2,1,0:T(8,128)S(1)}, bf16[64,9,16,128]{3,2,1,0:T(8,128)(2,1)S(1)}) custom-call(s32[880]{0:T(1024)S(1)} %copy-done.1, f32[4,64,128]{2,1,0:T(8,128)S(1)} %bitcast.24), custom_call_target="tpu_custom_call" | custom-call | flops 576716800 | bytes 1048576 | tf_op jit(solution)/shard_map/pull_own/pallas_call | solution.py:309
  160.1 0.0 collective-permute-done.8
  160.1 0.0 collective-permute-done.7
  160.3 0.1 collective-permute-start.12
  160.4 1.9 collective-permute-start.9
  162.3 0.1 maximum_maximum_fusion.1
  162.3 1.2 collective-permute-start.11
  163.6 0.8 collective-permute-start.10
  164.5 0.1 collective-permute-start.13
  164.5 69.0 %pull_caps.3.refs_8_ = f32[3,64,128]{2,1,0:T(8,128)S(1)} custom-call(s32[880]{0:T(1024)S(1)} %copy-done.1, f32[4,64,128]{2,1,0:T(8,128)S(1)} %bitcast.25, f32[4,32,128]{2,1,0:T(8,128)S(1)} %bitcast.28, f32[4,32,128]{2,1,0:T(8,128)S(1)} %bitcast.27, bf16[64,9,16,128]{3,2,1,0:T(8,128)(2,1)S(1)} %get-tuple-element.41.refs_4_.refs_7_, ...), custom_call_target="tpu_custom_call" | custom-call | flops 288358400 | bytes 1048576 | tf_op jit(solution)/shard_map/pull_caps/pallas_call | solution.py:309
  233.6 0.0 collective-permute-done.12
  233.6 0.0 collective-permute-done.13
  233.6 0.0 collective-permute-done.11
  233.6 0.0 collective-permute-done.10
  233.6 42.6 %pull_rim.3 = f32[3,64,128]{2,1,0:T(8,128)S(1)} custom-call(s32[272]{0:T(512)S(1)} %copy-done.2, f32[4,64,128]{2,1,0:T(8,128)S(1)} %bitcast.26, f32[4,32,128]{2,1,0:T(8,128)S(1)} %bitcast.31, f32[4,32,128]{2,1,0:T(8,128)S(1)} %bitcast.35, f32[4,32,128]{2,1,0:T(8,128)S(1)} %bitcast.33, f32[4,8,128]{2,1,0:T(8,128)S(1)} %bitcast.37, f32[4,8,128]{2,1,0:T(8,128)S(1)} %bitcast.39, ...), custom_call_target="tpu_custom_call" | custom-call | flops 267386880 | bytes 1048576 | tf_op jit(solution)/shard_map/pull_rim/pallas_call | solution.py:309
  276.2 0.8 add_select_fusion
  (33 shorter events, 0.6 us)
Async XLA Ops:
  2.7 26.6 %collective-permute-start.1 = (f32[4,8,4,1,128]{4,3,2,1,0:T(1,128)S(1)}, f32[4,8,4,1,128]{4,3,2,1,0:T(1,128)S(1)}, u32[]{:S(2)}, u32[]{:S(2)}) collective-permute-start(f32[4,8,4,1,128]{4,3,2,1,0:T(1,128)S(1)} %get-tuple-element.67), channel_id=1, source_target_pairs={{0,3},{1,0},{2,1},{3,2},{4,7},{5,4},{6,5},{7,6},{8,11},{9,8},{10,9... | collective-permute-start | bytes 196616 | tf_op jit(solution)/shard_map/ppermute | solution.py:335
  6.1 23.2 %collective-permute-start = (f32[4,8,4,1,128]{4,3,2,1,0:T(1,128)S(1)}, f32[4,8,4,1,128]{4,3,2,1,0:T(1,128)S(1)}, u32[]{:S(2)}, u32[]{:S(2)}) collective-permute-start(f32[4,8,4,1,128]{4,3,2,1,0:T(1,128)S(1)} %get-tuple-element.68), channel_id=1, source_target_pairs={{0,1},{1,2},{2,3},{3,0},{4,5},{5,6},{6,7},{7,4},{8,9},{9,10},{10,1... | collective-permute-start | bytes 196616 | tf_op jit(solution)/shard_map/ppermute | solution.py:335
  6.3 0.7 copy-start
  29.4 15.7 %collective-permute-start.5 = (f32[4,2,1,4,128]{4,3,2,1,0:T(4,128)S(1)}, f32[4,2,1,4,128]{4,3,2,1,0:T(4,128)S(1)}, u32[]{:S(2)}, u32[]{:S(2)}) collective-permute-start(f32[4,2,1,4,128]{4,3,2,1,0:T(4,128)S(1)} %maximum_maximum_fusion.2), channel_id=1, source_target_pairs={{0,20},{4,24},{8,28},{12,16},{16,4},{20,8},{24,12},{28,0},{1,21},{... | collective-permute-start | bytes 49160 | tf_op jit(solution)/shard_map/ppermute | solution.py:335
  31.5 13.6 %collective-permute-start.2 = (f32[4,8,1,4,128]{4,3,2,1,0:T(4,128)S(1)}, f32[4,8,1,4,128]{4,3,2,1,0:T(4,128)S(1)}, u32[]{:S(2)}, u32[]{:S(2)}) collective-permute-start(f32[4,8,1,4,128]{4,3,2,1,0:T(4,128)S(1)} %pad_maximum_fusion.2), channel_id=1, source_target_pairs={{0,4},{4,8},{8,12},{12,0},{1,5},{5,9},{9,13},{13,1},{2,6},{6,10},{... | collective-permute-start | bytes 196616 | tf_op jit(solution)/shard_map/ppermute | solution.py:335
  31.7 13.5 %collective-permute-start.4 = (f32[4,2,4,4,128]{4,3,2,1,0:T(4,128)S(1)}, f32[4,2,4,4,128]{4,3,2,1,0:T(4,128)S(1)}, u32[]{:S(2)}, u32[]{:S(2)}) collective-permute-start(f32[4,2,4,4,128]{4,3,2,1,0:T(4,128)S(1)} %maximum_maximum_fusion), channel_id=1, source_target_pairs={{0,16},{16,0},{1,17},{17,1},{2,18},{18,2},{3,19},{19,3},{4,20},{20... | collective-permute-start | bytes 196616 | tf_op jit(solution)/shard_map/ppermute | solution.py:335
  33.0 12.2 %collective-permute-start.3 = (f32[4,8,1,4,128]{4,3,2,1,0:T(4,128)S(1)}, f32[4,8,1,4,128]{4,3,2,1,0:T(4,128)S(1)}, u32[]{:S(2)}, u32[]{:S(2)}) collective-permute-start(f32[4,8,1,4,128]{4,3,2,1,0:T(4,128)S(1)} %pad_maximum_fusion.3), channel_id=1, source_target_pairs={{0,12},{4,0},{8,4},{12,8},{1,13},{5,1},{9,5},{13,9},{2,14},{6,2},{... | collective-permute-start | bytes 196616 | tf_op jit(solution)/shard_map/ppermute | solution.py:335
  33.9 11.3 %collective-permute-start.6 = (f32[4,2,1,4,128]{4,3,2,1,0:T(4,128)S(1)}, f32[4,2,1,4,128]{4,3,2,1,0:T(4,128)S(1)}, u32[]{:S(2)}, u32[]{:S(2)}) collective-permute-start(f32[4,2,1,4,128]{4,3,2,1,0:T(4,128)S(1)} %maximum_maximum_fusion.3), channel_id=1, source_target_pairs={{0,28},{4,16},{8,20},{12,24},{16,12},{20,0},{24,4},{28,8},{1,29},{... | collective-permute-start | bytes 49160 | tf_op jit(solution)/shard_map/ppermute | solution.py:335
  34.1 11.2 %copy-start.2 = (s32[272]{0:T(512)S(1)}, s32[272]{0:T(512)}, u32[]{:S(2)}) copy-start(s32[272]{0:T(512)} %constant.15.clone.refs_0_) | copy-start | bytes 3268
  45.2 11.6 %copy-start.3 = (f32[3,8,4,2,128]{4,3,2,1,0:T(2,128)S(1)}, f32[3,8,4,2,128]{4,3,2,1,0:T(2,128)}, u32[]{:S(2)}) copy-start(f32[3,8,4,2,128]{4,3,2,1,0:T(2,128)} %param.10) | copy-start | bytes 294916
  45.2 11.6 %copy-start.4 = (f32[3,8,4,2,128]{4,3,2,1,0:T(2,128)S(1)}, f32[3,8,4,2,128]{4,3,2,1,0:T(2,128)}, u32[]{:S(2)}) copy-start(f32[3,8,4,2,128]{4,3,2,1,0:T(2,128)} %param.11) | copy-start | bytes 294916
  45.2 15.6 %copy-start.1 = (s32[880]{0:T(1024)S(1)}, s32[880]{0:T(1024)}, u32[]{:S(2)}) copy-start(s32[880]{0:T(1024)} %constant.14.clone.refs_0_) | copy-start | bytes 10564
  57.2 102.9 %collective-permute-start.8 = (f32[4,8,4,1,128]{4,3,2,1,0:T(1,128)S(1)}, f32[4,8,4,1,128]{4,3,2,1,0:T(1,128)S(1)}, u32[]{:S(2)}, u32[]{:S(2)}) collective-permute-start(f32[4,8,4,1,128]{4,3,2,1,0:T(1,128)S(1)} %get-tuple-element.57), channel_id=1, source_target_pairs={{0,3},{1,0},{2,1},{3,2},{4,7},{5,4},{6,5},{7,6},{8,11},{9,8},{10,9... | collective-permute-start | bytes 196616 | tf_op jit(solution)/shard_map/ppermute | solution.py:335
  60.8 99.3 %collective-permute-start.7 = (f32[4,8,4,1,128]{4,3,2,1,0:T(1,128)S(1)}, f32[4,8,4,1,128]{4,3,2,1,0:T(1,128)S(1)}, u32[]{:S(2)}, u32[]{:S(2)}) collective-permute-start(f32[4,8,4,1,128]{4,3,2,1,0:T(1,128)S(1)} %get-tuple-element.58), channel_id=1, source_target_pairs={{0,1},{1,2},{2,3},{3,0},{4,5},{5,6},{6,7},{7,4},{8,9},{9,10},{10,1... | collective-permute-start | bytes 196616 | tf_op jit(solution)/shard_map/ppermute | solution.py:335
  160.3 73.3 %collective-permute-start.12 = (f32[4,2,1,4,128]{4,3,2,1,0:T(4,128)S(1)}, f32[4,2,1,4,128]{4,3,2,1,0:T(4,128)S(1)}, u32[]{:S(2)}, u32[]{:S(2)}) collective-permute-start(f32[4,2,1,4,128]{4,3,2,1,0:T(4,128)S(1)} %maximum_maximum_fusion.4), channel_id=1, source_target_pairs={{0,20},{4,24},{8,28},{12,16},{16,4},{20,8},{24,12},{28,0},{1,21},{... | collective-permute-start | bytes 49160 | tf_op jit(solution)/shard_map/ppermute | solution.py:335
  160.4 73.2 %collective-permute-start.9 = (f32[4,8,1,4,128]{4,3,2,1,0:T(4,128)S(1)}, f32[4,8,1,4,128]{4,3,2,1,0:T(4,128)S(1)}, u32[]{:S(2)}, u32[]{:S(2)}) collective-permute-start(f32[4,8,1,4,128]{4,3,2,1,0:T(4,128)S(1)} %pad_maximum_fusion.4), channel_id=1, source_target_pairs={{0,4},{4,8},{8,12},{12,0},{1,5},{5,9},{9,13},{13,1},{2,6},{6,10},{... | collective-permute-start | bytes 196616 | tf_op jit(solution)/shard_map/ppermute | solution.py:335
  162.3 71.3 %collective-permute-start.11 = (f32[4,2,4,4,128]{4,3,2,1,0:T(4,128)S(1)}, f32[4,2,4,4,128]{4,3,2,1,0:T(4,128)S(1)}, u32[]{:S(2)}, u32[]{:S(2)}) collective-permute-start(f32[4,2,4,4,128]{4,3,2,1,0:T(4,128)S(1)} %maximum_maximum_fusion.1), channel_id=1, source_target_pairs={{0,16},{16,0},{1,17},{17,1},{2,18},{18,2},{3,19},{19,3},{4,20},{20... | collective-permute-start | bytes 196616 | tf_op jit(solution)/shard_map/ppermute | solution.py:335
  163.6 70.0 %collective-permute-start.10 = (f32[4,8,1,4,128]{4,3,2,1,0:T(4,128)S(1)}, f32[4,8,1,4,128]{4,3,2,1,0:T(4,128)S(1)}, u32[]{:S(2)}, u32[]{:S(2)}) collective-permute-start(f32[4,8,1,4,128]{4,3,2,1,0:T(4,128)S(1)} %pad_maximum_fusion.5), channel_id=1, source_target_pairs={{0,12},{4,0},{8,4},{12,8},{1,13},{5,1},{9,5},{13,9},{2,14},{6,2},{... | collective-permute-start | bytes 196616 | tf_op jit(solution)/shard_map/ppermute | solution.py:335
  164.5 69.1 %collective-permute-start.13 = (f32[4,2,1,4,128]{4,3,2,1,0:T(4,128)S(1)}, f32[4,2,1,4,128]{4,3,2,1,0:T(4,128)S(1)}, u32[]{:S(2)}, u32[]{:S(2)}) collective-permute-start(f32[4,2,1,4,128]{4,3,2,1,0:T(4,128)S(1)} %maximum_maximum_fusion.5), channel_id=1, source_target_pairs={{0,28},{4,16},{8,20},{12,24},{16,12},{20,0},{24,4},{28,8},{1,29},{... | collective-permute-start | bytes 49160 | tf_op jit(solution)/shard_map/ppermute | solution.py:335
